TPU v7x, 32 devices: a whole 2x2x4 slice. The times are simulated.
32 devices in a mesh: parts: 2 (over y), row: 16 (over z, x, core).
Axes of the slice: x: 2, y: 2, z: 4, core: 2. Of those that a mesh axis runs over, the one named last changes fastest.
Arguments:
- tokens: bfloat16 [64, 256, 768], P(('parts', 'row')), parts along dimension 0, may hold values from -6 to 6
- w_query: bfloat16 [768, 768], replicated, may hold values from -0.21875 to 0.21875
- w_key: bfloat16 [768, 768], replicated, may hold values from -0.21875 to 0.21875
- w_value: bfloat16 [768, 768], replicated, may hold values from -0.21875 to 0.21875
- w_out: bfloat16 [768, 768], replicated, may hold values from -0.21875 to 0.21875
- omega: bfloat16 [12, 64, 256], replicated, may hold values from -5 to 5
- conv_kernel: float32 [3, 3, 768], replicated, may hold values from -0.6 to 0.6
- norm_gain: float32 [768], replicated, may hold values from 0.1 to 1.9
Outputs:
- layer_out: bfloat16 [64, 256, 768], P(('parts', 'row')), parts along dimension 0
There are 2 independent parts, one for each index of `parts`. A program takes and returns all parts, laid end to end along the dimension named above; an argument that names none is the same for every part. Nothing has to cross between parts.
All inputs are finite; a program needn't handle non-finite values.
Results may differ from a plain program's by a relative error of at most 0.0081.
Values may be sent and summed in bfloat16 or wider, within the bound.
A program may use at most 64 MiB of HBM per device.

v0:
```python
import jax
import jax.numpy as jnp
from jax import lax
from jax.sharding import PartitionSpec as P


def with_halo(block, sides, width):
    for axis, dim in sides:
        count = lax.axis_size(axis)
        forward = [(i, i + 1) for i in range(count - 1)]
        backward = [(target, source) for source, target in forward]
        low = lax.ppermute(
            lax.slice_in_dim(block, block.shape[dim] - width, None, axis=dim), axis, forward
        )
        high = lax.ppermute(lax.slice_in_dim(block, 0, width, axis=dim), axis, backward)
        block = jnp.concatenate([low, block, high], axis=dim)
    return block


def project(rows, weight):
    return jnp.dot(rows, weight, preferred_element_type=jnp.float32).astype(jnp.bfloat16)


def feature_map(heads_in, omega):
    dim_head = heads_in.shape[-1]
    lifted = jnp.einsum("thd,hdf->thf", heads_in, omega, preferred_element_type=jnp.float32)
    values = heads_in.astype(jnp.float32)
    square = jnp.sum(values * values, axis=-1, keepdims=True)
    feats = jnp.exp(lifted * dim_head ** (-0.25) - square * 0.5 * dim_head ** (-0.5)) * omega.shape[
        -1
    ] ** (-0.5)
    return feats.astype(jnp.bfloat16)


def shards(tokens, w_query, w_key, w_value, w_out, omega, conv_kernel, norm_gain):
    rows_here, cols, width = tokens.shape
    heads, dim_head, nfeat = omega.shape
    flat = tokens.reshape(rows_here * cols, width)
    value = project(flat, w_value)
    value_ext = with_halo(value.reshape(rows_here, cols, width), (("row", 0),), 1)
    feat_key = feature_map(project(flat, w_key).reshape(-1, heads, dim_head), omega)
    local_state = jnp.einsum(
        "thf,thd->fhd",
        feat_key,
        value.reshape(-1, heads, dim_head),
        preferred_element_type=jnp.float32,
    )
    local_sum = jnp.sum(feat_key.astype(jnp.float32), axis=0)
    feat_query = feature_map(project(flat, w_query).reshape(-1, heads, dim_head), omega)
    padded = jnp.pad(value_ext.astype(jnp.float32), ((0, 0), (1, 1), (0, 0)))
    position = jnp.zeros((rows_here, cols, width), jnp.float32)
    for shift_a in range(3):
        for shift_b in range(3):
            position = (
                position
                + padded[shift_a : shift_a + rows_here, shift_b : shift_b + cols, :]
                * conv_kernel[shift_a, shift_b]
            )
    kv_sum, key_sum = lax.psum((local_state.reshape(nfeat, width), local_sum), "row")
    kv_state = kv_sum.astype(jnp.bfloat16).reshape(nfeat, heads, dim_head)
    numer = jnp.einsum("thf,fhd->thd", feat_query, kv_state, preferred_element_type=jnp.float32)
    denom = jnp.einsum(
        "thf,hf->th", feat_query.astype(jnp.float32), key_sum, precision=lax.Precision.HIGHEST
    )
    attn = numer / denom[:, :, None]
    scale = lax.rsqrt(jnp.mean(attn * attn, axis=(1, 2), keepdims=True) + 1e-06)
    normed = (attn * scale).reshape(-1, width) * norm_gain
    mixed = (normed + position.reshape(-1, width)).astype(jnp.bfloat16)
    out = flat.astype(jnp.float32) + jnp.dot(mixed, w_out, preferred_element_type=jnp.float32)
    return out.astype(jnp.bfloat16).reshape(rows_here, cols, width)


def solution(mesh):
    return jax.shard_map(
        shards,
        mesh=mesh,
        in_specs=(P(("parts", "row"), None, None), P(), P(), P(), P(), P(), P(), P()),
        out_specs=P(("parts", "row"), None, None),
        check_vma=False,
    )
```

profile of v0, /device:TPU:0, one launch (start us, length us, event | category | flops | bytes accessed | tf_op | source)
XLA Modules:
  0.0 115.2 jit_solution(12742287627702785171)
XLA Ops:
  0.0 0.0 copy-start
  0.0 1.3 %copy-done = bf16[768,768]{1,0:T(8,128)(2,1)S(1)} copy-done((bf16[768,768]{1,0:T(8,128)(2,1)S(1)}, bf16[768,768]{1,0:T(8,128)(2,1)}, u32[]{:S(2)}) %copy-start) | copy-done | bytes 1179672
  1.3 1.9 %convolution_convert_fusion.2 = bf16[512,768]{1,0:T(8,128)(2,1)S(1)} fusion(bf16[512,768]{1,0:T(8,128)(2,1)} %bitcast.72, bf16[768,768]{1,0:T(8,128)(2,1)S(1)} %copy-done), kind=kOutput, calls=%fused_computation.43 | convolution fusion | flops 604372992 | bytes 2752512 | tf_op jit(solution)/shard_map/dot_general | solution.py:21
  3.2 0.0 copy-start.6
  3.2 0.9 slice_bitcast_fusion.1
  4.1 3.1 %collective-permute-start = (bf16[1,256,768]{2,1,0:T(8,128)(2,1)}, bf16[1,256,768]{2,1,0:T(8,128)(2,1)}, u32[]{:S(2)}, u32[]{:S(2)}) collective-permute-start(bf16[1,256,768]{2,1,0:T(8,128)(2,1)} %get-tuple-element.16), channel_id=1, source_target_pairs={{0,1},{1,2},{2,3},{3,4},{4,5},{5,6},{6,7},{7,8},{8,9},{9,10},{10,1... | collective-permute-start | bytes 1179656 | tf_op jit(solution)/shard_map/ppermute | solution.py:12
  7.3 1.3 %collective-permute-start.1 = (bf16[1,256,768]{2,1,0:T(8,128)(2,1)}, bf16[1,256,768]{2,1,0:T(8,128)(2,1)}, u32[]{:S(2)}, u32[]{:S(2)}) collective-permute-start(bf16[1,256,768]{2,1,0:T(8,128)(2,1)} %get-tuple-element.17), channel_id=1, source_target_pairs={{1,0},{2,1},{3,2},{4,3},{5,4},{6,5},{7,6},{8,7},{9,8},{10,9},{11,1... | collective-permute-start | bytes 1179656 | tf_op jit(solution)/shard_map/ppermute | solution.py:15
  8.6 0.3 copy.13
  8.8 0.0 copy-done.6
  8.9 2.9 %convolution_convert_fusion.1 = bf16[512,768]{1,0:T(8,128)(2,1)} fusion(bf16[512,768]{1,0:T(8,128)(2,1)S(1)} %bitcast.73, bf16[768,768]{1,0:T(8,128)(2,1)} %param.10), kind=kOutput, calls=%fused_computation.42 | convolution fusion | flops 604372992 | bytes 2752512 | tf_op jit(solution)/shard_map/dot_general | solution.py:21
  11.8 1.4 %copy.14 = bf16[512,768]{0,1:T(8,128)(2,1)S(1)} copy(bf16[512,768]{1,0:T(8,128)(2,1)} %convolution_convert_fusion.1) | data formatting | bytes 1572864 | tf_op jit(solution)/shard_map/convert_element_type | solution.py:21
  13.2 0.2 multiply_reduce_fusion.2
  13.4 3.2 %convert_reduce_fusion = (f32[12,256]{1,0:T(8,128)S(1)}, bf16[512,12,256]{2,0,1:T(8,128)(2,1)S(1)}) fusion(f32[512,12]{0,1:T(8,128)S(1)} %broadcast_multiply_fusion.2, bf16[512,12,64]{0,2,1:T(8,128)(2,1)S(1)} %bitcast.67, bf16[12,64,256]{2,1,0:T(8,128)(2,1)} %param.13), kind=kOutput, calls=%fused_computation.8 | convolution fusion | flops 210760704 | bytes 4362240 | tf_op jit(solution)/shard_map/thd,hdf->thf/dot_general | solution.py:26
  16.7 0.0 copy-start.4
  16.7 0.0 copy-start.7
  16.7 0.7 fusion.24
  17.3 0.6 copy-done.4
  17.9 0.2 copy-done.7
  18.2 1.7 %convolution_convert_fusion = bf16[512,768]{1,0:T(8,128)(2,1)} fusion(bf16[512,768]{1,0:T(8,128)(2,1)S(1)} %bitcast.74, bf16[768,768]{1,0:T(8,128)(2,1)S(1)} %copy-done.4), kind=kOutput, calls=%fused_computation.41 | convolution fusion | flops 604372992 | bytes 2752512 | tf_op jit(solution)/shard_map/dot_general | solution.py:21
  19.8 1.4 %copy.15 = bf16[512,768]{0,1:T(8,128)(2,1)S(1)} copy(bf16[512,768]{1,0:T(8,128)(2,1)} %convolution_convert_fusion) | data formatting | bytes 1572864 | tf_op jit(solution)/shard_map/convert_element_type | solution.py:21
  21.2 0.2 multiply_reduce_fusion.1
  21.4 4.1 %fusion.2 = bf16[512,12,256]{2,0,1:T(8,128)(2,1)} fusion(f32[512,12]{0,1:T(8,128)S(1)} %broadcast_multiply_fusion.1, bf16[512,12,64]{0,2,1:T(8,128)(2,1)S(1)} %bitcast.69, bf16[12,64,256]{2,1,0:T(8,128)(2,1)} %param.13), kind=kOutput, calls=%fused_computation.3 | convolution fusion | flops 207618048 | bytes 4349952 | tf_op jit(solution)/shard_map/thd,hdf->thf/dot_general | solution.py:26
  25.6 73.0 %all-reduce.3 = (bf16[256,768]{0,1:T(8,128)(2,1)S(1)}, f32[12,256]{1,0:T(8,128)S(1)}) all-reduce(f32[256,768]{0,1:T(8,128)S(1)} %bitcast.64, f32[12,256]{1,0:T(8,128)S(1)} %get-tuple-element.18), channel_id=1, replica_groups=mesh['parts'=2,'row'=16] {'row'}, use_global_device_ids=true, to_apply=%region_1.0 | all-reduce | flops 199680 | bytes 1204224 | tf_op jit(solution)/shard_map/psum | solution.py:59
  98.6 0.0 copy-start.1
  98.6 4.6 %fusion.22 = f32[12,1,512]{2,1,0:T(1,128)S(1)} fusion(bf16[512,12,256]{2,0,1:T(8,128)(2,1)} %fusion.2, f32[12,256,1]{1,0,2:T(8,128)S(1)} %bitcast.71), kind=kOutput, calls=%fused_computation.50 | convolution fusion | flops 18874368 | bytes 3182592 | tf_op jit(solution)/shard_map/thf,hf->th/dot_general | solution.py:62
  103.2 0.0 copy-done.1
  103.2 0.0 copy-start.2
  103.2 1.1 multiply_reduce_fusion
  104.4 0.0 copy-done.2
  104.4 0.1 slice_reduce_fusion.8
  104.4 1.3 %broadcast_multiply_fusion = f32[512,12,64]{0,2,1:T(8,128)} fusion(f32[512,12,64]{0,2,1:T(8,128)S(1)} %get-tuple-element.21, f32[512]{0:T(512)S(1)} %add_rsqrt_fusion), kind=kLoop, calls=%fused_computation.44 | loop fusion | flops 393216 | bytes 3147776 | tf_op jit(solution)/shard_map/mul | solution.py:67
  105.8 0.0 collective-permute-done
  105.8 0.0 collective-permute-done.1
  105.8 1.4 %maximum_convert_fusion = f32[4,256,768]{2,1,0:T(8,128)S(1)} fusion(bf16[1,256,768]{2,1,0:T(8,128)(2,1)} %collective-permute-done.1, bf16[2,256,768]{2,1,0:T(8,128)(2,1)S(1)} %bitcast.62, bf16[1,256,768]{2,1,0:T(8,128)(2,1)} %collective-permute-done), kind=kLoop, calls=%fused_computation.32 | loop fusion | flops 2359296 | bytes 4718592 | tf_op jit(solution)/shard_map/convert_element_type | solution.py:50
  107.1 2.5 %fusion.14 = f32[2,256,768]{2,1,0:T(8,128)} fusion(f32[4,256,768]{2,1,0:T(8,128)S(1)} %maximum_convert_fusion, f32[768]{0:T(1024)S(1)} %get-tuple-element.12, f32[768]{0:T(1024)S(1)} %get-tuple-element.13, f32[768]{0:T(1024)S(1)} %get-tuple-element.6, f32[768]{0:T(1024)S(1)} %get-tuple-element.7, f32[768]{0:T(1024)S(1)} %get-tuple-element.8, ...), kind=kLoop, calls=%fused_computation.23 | loop fusion | flops 6684672 | bytes 9474048 | tf_op jit(solution)/shard_map/add | solution.py:55
  109.6 0.0 copy-start.3
  109.6 1.9 %copy.16 = f32[512,768]{0,1:T(8,128)S(1)} copy(f32[512,768]{1,0:T(8,128)} %bitcast.63) | data formatting | bytes 3145728 | tf_op jit(solution)/shard_map/reshape | solution.py:68
  111.5 0.0 copy-done.3
  111.5 0.0 copy-start.5
  111.5 0.0 copy-start.8
  111.6 1.7 %fusion.21 = bf16[512,768]{0,1:T(8,128)(2,1)S(1)} fusion(f32[512,768]{0,1:T(8,128)S(1)} %copy.16, f32[512,12,64]{0,2,1:T(8,128)} %broadcast_multiply_fusion, f32[768]{0:T(1024)S(1)} %copy-done.3), kind=kLoop, calls=%fused_computation.35 | loop fusion | flops 1179648 | bytes 3935232 | tf_op jit(solution)/shard_map/convert_element_type | solution.py:68
  113.3 0.0 copy-done.5
  113.3 0.2 copy-done.8
  113.5 1.7 %add_convert_fusion = bf16[512,768]{1,0:T(8,128)(2,1)} fusion(bf16[512,768]{1,0:T(8,128)(2,1)S(1)} %bitcast.75, bf16[512,768]{0,1:T(8,128)(2,1)S(1)} %fusion.21, bf16[768,768]{1,0:T(8,128)(2,1)S(1)} %copy-done.5), kind=kOutput, calls=%fused_computation.37 | convolution fusion | flops 605159424 | bytes 3538944 | tf_op jit(solution)/shard_map/dot_general | solution.py:69
  (4 shorter events, 0.0 us)
Async XLA Ops:
  0.0 1.3 %copy-start = (bf16[768,768]{1,0:T(8,128)(2,1)S(1)}, bf16[768,768]{1,0:T(8,128)(2,1)}, u32[]{:S(2)}) copy-start(bf16[768,768]{1,0:T(8,128)(2,1)} %param.11) | copy-start | bytes 3538948
  3.2 5.7 %copy-start.6 = (bf16[2,256,768]{2,1,0:T(8,128)(2,1)S(1)}, bf16[2,256,768]{2,1,0:T(8,128)(2,1)}, u32[]{:S(2)}) copy-start(bf16[2,256,768]{2,1,0:T(8,128)(2,1)} %param.8) | copy-start | bytes 2359300
  4.1 101.6 %collective-permute-start = (bf16[1,256,768]{2,1,0:T(8,128)(2,1)}, bf16[1,256,768]{2,1,0:T(8,128)(2,1)}, u32[]{:S(2)}, u32[]{:S(2)}) collective-permute-start(bf16[1,256,768]{2,1,0:T(8,128)(2,1)} %get-tuple-element.16), channel_id=1, source_target_pairs={{0,1},{1,2},{2,3},{3,4},{4,5},{5,6},{6,7},{7,8},{8,9},{9,10},{10,1... | collective-permute-start | bytes 1179656 | tf_op jit(solution)/shard_map/ppermute | solution.py:12
  7.3 98.5 %collective-permute-start.1 = (bf16[1,256,768]{2,1,0:T(8,128)(2,1)}, bf16[1,256,768]{2,1,0:T(8,128)(2,1)}, u32[]{:S(2)}, u32[]{:S(2)}) collective-permute-start(bf16[1,256,768]{2,1,0:T(8,128)(2,1)} %get-tuple-element.17), channel_id=1, source_target_pairs={{1,0},{2,1},{3,2},{4,3},{5,4},{6,5},{7,6},{8,7},{9,8},{10,9},{11,1... | collective-permute-start | bytes 1179656 | tf_op jit(solution)/shard_map/ppermute | solution.py:15
  16.7 1.3 %copy-start.4 = (bf16[768,768]{1,0:T(8,128)(2,1)S(1)}, bf16[768,768]{1,0:T(8,128)(2,1)}, u32[]{:S(2)}) copy-start(bf16[768,768]{1,0:T(8,128)(2,1)} %param.9) | copy-start | bytes 3538948
  16.7 1.5 %copy-start.7 = (bf16[2,256,768]{2,1,0:T(8,128)(2,1)S(1)}, bf16[2,256,768]{2,1,0:T(8,128)(2,1)}, u32[]{:S(2)}) copy-start(bf16[2,256,768]{2,1,0:T(8,128)(2,1)} %param.8) | copy-start | bytes 2359300
  98.6 4.6 %copy-start.1 = (bf16[512,12,256]{2,0,1:T(8,128)(2,1)S(1)}, bf16[512,12,256]{2,0,1:T(8,128)(2,1)}, u32[]{:S(2)}) copy-start(bf16[512,12,256]{2,0,1:T(8,128)(2,1)} %fusion.2) | copy-start | bytes 9437188
  103.2 1.1 copy-start.2
  109.6 1.9 %copy-start.3 = (f32[768]{0:T(1024)S(1)}, f32[768]{0:T(1024)}, u32[]{:S(2)}) copy-start(f32[768]{0:T(1024)} %param.15) | copy-start | bytes 9220
  111.5 1.8 %copy-start.5 = (bf16[768,768]{1,0:T(8,128)(2,1)S(1)}, bf16[768,768]{1,0:T(8,128)(2,1)}, u32[]{:S(2)}) copy-start(bf16[768,768]{1,0:T(8,128)(2,1)} %param.12) | copy-start | bytes 3538948
  111.5 2.0 %copy-start.8 = (bf16[2,256,768]{2,1,0:T(8,128)(2,1)S(1)}, bf16[2,256,768]{2,1,0:T(8,128)(2,1)}, u32[]{:S(2)}) copy-start(bf16[2,256,768]{2,1,0:T(8,128)(2,1)} %param.8) | copy-start | bytes 2359300
where the time goes:
time: 116 us; the launch traced here: 115 us
  blocking collectives  73 us (63%)
  matrix products  21.9 us (19%)
  local copies, waits for them, and re-layouts  8.3 us (7%)
  other arithmetic  7.33 us (6%)
  starting transfers between devices  4.42 us (4%)
    psum x1, blocking collectives, shards(): lax.psum((local_state.reshape(nfeat, width), local_sum), 'row')  73 us
    dot_general x2, matrix products, feature_map(): jnp.einsum('thd,hdf->thf', heads_in, omega, preferred_element_type=jnp.fl...  7.36 us
    dot_general x3, matrix products, project(): jnp.dot(rows, weight, preferred_element_type=jnp.float32)  6.5 us
    dot_general x1, matrix products, shards(): jnp.einsum('thf,hf->th', feat_query.astype(jnp.float32), key_sum, precisi...  4.57 us
    ppermute x1, starting transfers between devices, with_halo(): lax.ppermute(lax.slice_in_dim(block, block.shape[dim] - width, None, axis...  3.14 us
    convert_element_type x3, local copies, waits for them, and re-layouts, project(): jnp.dot(rows, weight, preferred_element_type=jnp.float32)  3.1 us
    add x1, other arithmetic, shards(): position + padded[shift_a:shift_a + rows_here, shift_b:shift_b + cols, :]...  2.48 us
  transfers between devices with their start and end apart: 2, of which 0 were waited for; matrix products, arithmetic and copies ran while one was open for 20% of the time, Pallas kernels for 0%

commit v1 on v0

--- a/solution.py
+++ b/solution.py
@@ -1,7 +1,15 @@
+import functools
+import math
+
 import jax
 import jax.numpy as jnp
 from jax import lax
+from jax.experimental import pallas as pl
+from jax.experimental.pallas import tpu as pltpu
 from jax.sharding import PartitionSpec as P
+
+F32, BF16 = jnp.float32, jnp.bfloat16
+LANES, SUB = 128, 16
 
 
 def with_halo(block, sides, width):
@@ -70,9 +78,331 @@
     return out.astype(jnp.bfloat16).reshape(rows_here, cols, width)
 
 
+def mm(a, b):
+    return jnp.dot(a, b, preferred_element_type=F32)
+
+
+def kernel(
+    dims,
+    tok_hbm, wq_hbm, wk_hbm, wv_hbm, wo_hbm, om_hbm, conv_ref, gain_ref,
+    out_hbm,
+    tok, wq, wk, wv, wo, om, val, halo, fq, pos, att, outv,
+    stf, kst, d2d_src, d2d_dst, rs_src, rs_dst, fin,
+    load_sem, out_sem, halo_s, halo_r, d2d_s, d2d_r, rs_s, rs_r, ag_s, ag_r, fw_s, fw_r,
+):
+    n, rows_here, cols, width, heads, dh, nfeat, groups = dims
+    chips, half = n // 2, nfeat // 2
+    piece = half // chips
+    pairs = heads // 2
+    nrows = rows_here * cols
+    me = lax.axis_index("row")
+    chip, core = me // 2, me % 2
+    mate = me + 1 - 2 * core
+
+    loads = [
+        pltpu.make_async_copy(src, dst, load_sem.at[i])
+        for i, (src, dst) in enumerate(
+            [(tok_hbm, tok), (wv_hbm, wv), (wk_hbm, wk), (om_hbm, om), (wq_hbm, wq), (wo_hbm, wo)]
+        )
+    ]
+    for copy in loads:
+        copy.start()
+
+    barrier = pltpu.get_barrier_semaphore()
+    for d in range(1, n):
+        pl.semaphore_signal(
+            barrier, inc=1, device_id={"row": lax.rem(me + d, n)},
+            device_id_type=pl.DeviceIdType.MESH,
+        )
+
+    def remote(src, dst, s, r, target):
+        return pltpu.make_async_remote_copy(
+            src_ref=src, dst_ref=dst, send_sem=s, recv_sem=r,
+            device_id={"row": target}, device_id_type=pl.DeviceIdType.MESH,
+        )
+
+    lane_lo = lax.broadcasted_iota(jnp.int32, (1, LANES), 1) < dh
+    sq_scale = 0.5 * dh ** (-0.5) * dh ** 0.25
+    arg_scale = dh ** (-0.25)
+    arg_shift = 0.5 * math.log(nfeat)
+    minus = jnp.full((LANES, nfeat), -1.0, BF16)
+    zero_om = jnp.zeros((dh, nfeat), BF16)
+
+    def feats(u, pair):
+        uf = u.astype(F32)
+        sq = uf * uf * sq_scale
+        hi = sq.astype(BF16).astype(F32)
+        lo = pltpu.roll(sq - hi, dh, 1)
+        out = []
+        for k in range(2):
+            tail = jnp.where(lane_lo, hi, lo) if k == 0 else jnp.where(lane_lo, lo, hi)
+            lhs = jnp.concatenate([u, tail.astype(BF16)], axis=1)
+            o = om[2 * pair + k]
+            top = [o, zero_om] if k == 0 else [zero_om, o]
+            rhs = jnp.concatenate(top + [minus], axis=0)
+            out.append(jnp.exp(mm(lhs, rhs) * arg_scale - arg_shift).astype(BF16))
+        return out
+
+    loads[0].wait()
+    loads[1].wait()
+    t = tok[...]
+    for q in range(0, width, 2 * LANES):
+        val[:, q : q + 2 * LANES] = mm(t, wv[:, q : q + 2 * LANES]).astype(BF16)
+    pl.semaphore_wait(barrier, n - 1)
+    to_next = remote(val.at[pl.ds(nrows - cols, cols)], halo.at[0], halo_s.at[0], halo_r.at[0],
+                     lax.rem(me + 1, n))
+    to_prev = remote(val.at[pl.ds(0, cols)], halo.at[1], halo_s.at[1], halo_r.at[1],
+                     lax.rem(me + n - 1, n))
+
+    @pl.when(me < n - 1)
+    def _():
+        to_next.start()
+
+    @pl.when(me > 0)
+    def _():
+        to_prev.start()
+
+    own_rows = pl.ds(pl.multiple_of(core * half, half), half)
+    mate_rows = pl.ds(pl.multiple_of((1 - core) * half, half), half)
+    d2d = [
+        remote(d2d_src.at[s], d2d_dst.at[s], d2d_s.at[s], d2d_r.at[s], mate)
+        for s in range(pairs + 1)
+    ]
+
+    def put_slab(s, block):
+        stf[s] = block
+        d2d_src[s] = stf[s, mate_rows, :].astype(BF16)
+        d2d[s].start()
+
+    kst[...] = jnp.zeros_like(kst)
+    ones = jnp.ones((SUB, nrows), BF16)
+
+    def key_quad(g):
+        u2 = mm(t, wk[:, 2 * LANES * g : 2 * LANES * (g + 1)]).astype(BF16)
+        for i in range(2):
+            pair = 2 * g + i
+            f0, f1 = feats(u2[:, LANES * i : LANES * (i + 1)], pair)
+            vt = val[:, LANES * pair : LANES * (pair + 1)].T
+            lhs = jnp.concatenate([vt, ones], axis=0)
+            s0, s1 = mm(lhs, f0), mm(lhs, f1)
+            kst[2 * pair : 2 * pair + 1, :] = s0[LANES : LANES + 1]
+            kst[2 * pair + 1 : 2 * pair + 2, :] = s1[LANES : LANES + 1]
+            put_slab(pair, jnp.concatenate([s0[:dh], s1[dh:LANES]], axis=0).T)
+
+    def query_quad(g):
+        u2 = mm(t, wq[:, 2 * LANES * g : 2 * LANES * (g + 1)]).astype(BF16)
+        for i in range(2):
+            pair = 2 * g + i
+            f0, f1 = feats(u2[:, LANES * i : LANES * (i + 1)], pair)
+            fq[2 * pair] = f0
+            fq[2 * pair + 1] = f1
+
+    rs, ag, fw = [], [], []
+    my_rows = pl.ds(pl.multiple_of(core * half + chip * piece, piece), piece)
+    for gi, (a, b) in enumerate(groups):
+        rs_g, ag_g = [], []
+        for d in range(1, chips):
+            peer = lax.rem(chip + d, chips)
+            rs_g.append(remote(rs_src.at[peer, a:b], rs_dst.at[d, a:b],
+                               rs_s.at[gi, d], rs_r.at[gi, d], 2 * peer + core))
+            ag_g.append(remote(fin.at[a:b, my_rows], fin.at[a:b, my_rows],
+                               ag_s.at[gi, d], ag_r.at[gi, d], 2 * peer + core))
+        rs.append(rs_g)
+        ag.append(ag_g)
+        fw_g = []
+        for d in range(chips):
+            source = lax.rem(chip + chips - d, chips)
+            rows = pl.ds(pl.multiple_of(core * half + source * piece, piece), piece)
+            fw_g.append(remote(fin.at[a:b, rows], fin.at[a:b, rows],
+                               fw_s.at[gi, d], fw_r.at[gi, d], mate))
+        fw.append(fw_g)
+
+    def scatter(gi):
+        a, b = groups[gi]
+        for s in range(a, b):
+            d2d[s].wait_recv()
+            both = stf[s, own_rows, :] + d2d_dst[s].astype(F32)
+            rs_src[:, s] = both.astype(BF16).reshape(chips, piece, LANES)
+        for copy in reversed(rs[gi]):
+            copy.start()
+
+    def gather(gi):
+        a, b = groups[gi]
+        total = rs_src[chip, a:b].astype(F32)
+        for d in range(1, chips):
+            rs[gi][d - 1].wait_recv()
+            total = total + rs_dst[d, a:b].astype(F32)
+        fin[a:b, my_rows, :] = total.astype(BF16)
+        for copy in reversed(ag[gi]):
+            copy.start()
+        fw[gi][0].start()
+
+    def forward(gi):
+        for d in range(1, chips):
+            ag[gi][d - 1].wait_recv()
+            fw[gi][d].start()
+
+    def convolve():
+        @pl.when(me < n - 1)
+        def _():
+            to_prev.wait_recv()
+
+        @pl.when(me > 0)
+        def _():
+            to_next.wait_recv()
+
+        @pl.when(me == n - 1)
+        def _():
+            halo[1] = jnp.zeros_like(halo[1])
+
+        @pl.when(me == 0)
+        def _():
+            halo[0] = jnp.zeros_like(halo[0])
+
+        col = lax.broadcasted_iota(jnp.int32, (cols, LANES), 0)
+        for q in range(0, width, LANES):
+            cut = slice(q, q + LANES)
+            lines = [halo[0, :, cut]]
+            lines += [val[r * cols : (r + 1) * cols, cut] for r in range(rows_here)]
+            lines += [halo[1, :, cut]]
+            lines = [x.astype(F32) for x in lines]
+            for r in range(rows_here):
+                acc = []
+                for b in range(3):
+                    part = lines[r] * conv_ref[0, b : b + 1, cut]
+                    for a in range(1, 3):
+                        part = part + lines[r + a] * conv_ref[a, b : b + 1, cut]
+                    acc.append(part)
+                left = jnp.where(col == 0, 0.0, pltpu.roll(acc[0], 1, 0))
+                right = jnp.where(col == cols - 1, 0.0, pltpu.roll(acc[2], cols - 1, 0))
+                pos[r * cols : (r + 1) * cols, cut] = acc[1] + left + right
+
+    loads[2].wait()
+    loads[3].wait()
+    key_quad(0)
+    key_quad(1)
+    scatter(0)
+    key_quad(2)
+    put_slab(pairs, kst[...].T)
+    loads[4].wait()
+    query_quad(0)
+    scatter(1)
+    query_quad(1)
+    gather(0)
+    query_quad(2)
+    gather(1)
+    convolve()
+    forward(0)
+    forward(1)
+    for gi in range(len(groups)):
+        for copy in fw[gi]:
+            copy.wait_recv()
+
+    ks = fin[pairs]
+    sumsq = jnp.zeros((nrows, LANES), F32)
+    pick_row = lax.broadcasted_iota(jnp.int32, (LANES, LANES), 0)
+    pick_lane = lax.broadcasted_iota(jnp.int32, (LANES, LANES), 1) // dh
+    zero = jnp.zeros((), BF16)
+    for p in range(pairs):
+        pick = jnp.where(pick_row == 2 * p + pick_lane, 1.0, 0.0).astype(BF16)
+        krep = mm(ks, pick).astype(BF16)
+        sp = fin[p]
+        lo = jnp.concatenate([jnp.where(lane_lo, sp, zero), jnp.where(lane_lo, krep, zero)], 1)
+        hi = jnp.concatenate([jnp.where(lane_lo, zero, sp), jnp.where(lane_lo, zero, krep)], 1)
+        both = mm(fq[2 * p], lo) + mm(fq[2 * p + 1], hi)
+        attn = both[:, :LANES] / both[:, LANES:]
+        att[:, LANES * p : LANES * (p + 1)] = attn
+        sumsq = sumsq + attn * attn
+    scale = lax.rsqrt(jnp.sum(sumsq, axis=1, keepdims=True) * (1.0 / width) + 1e-06)
+    loads[5].wait()
+    outs = []
+    for r in range(rows_here):
+        cut = slice(r * cols, (r + 1) * cols)
+        mixed = (att[cut] * scale[cut] * gain_ref[...] + pos[cut]).astype(BF16)
+        outv[cut] = (tok[cut].astype(F32) + mm(mixed, wo[...])).astype(BF16)
+        copy = pltpu.make_async_copy(outv.at[cut], out_hbm.at[cut], out_sem.at[r])
+        copy.start()
+        outs.append(copy)
+
+    @pl.when(me < n - 1)
+    def _():
+        to_next.wait_send()
+
+    @pl.when(me > 0)
+    def _():
+        to_prev.wait_send()
+
+    for copy in d2d:
+        copy.wait_send()
+    for gi in range(len(groups)):
+        for copy in rs[gi] + ag[gi] + fw[gi]:
+            copy.wait_send()
+    for copy in outs:
+        copy.wait()
+
+
+def fused(n, tokens, w_query, w_key, w_value, w_out, omega, conv_kernel, norm_gain):
+    rows_here, cols, width = tokens.shape
+    heads, dh, nfeat = omega.shape
+    nrows = rows_here * cols
+    chips, half, slabs = n // 2, nfeat // 2, heads // 2 + 1
+    piece = half // chips
+    groups = ((0, 4), (4, slabs))
+    dims = (n, rows_here, cols, width, heads, dh, nfeat, groups)
+    any_spec = pl.BlockSpec(memory_space=pl.ANY)
+    vmem_spec = pl.BlockSpec(memory_space=pltpu.VMEM)
+    sem = pltpu.SemaphoreType.DMA
+    ng = len(groups)
+    flat = tokens.reshape(nrows, width)
+    out = pl.pallas_call(
+        functools.partial(kernel, dims),
+        out_shape=jax.ShapeDtypeStruct((nrows, width), BF16),
+        in_specs=[any_spec] * 6 + [vmem_spec] * 2,
+        out_specs=any_spec,
+        scratch_shapes=[
+            pltpu.VMEM((nrows, width), BF16),
+            pltpu.VMEM((width, width), BF16),
+            pltpu.VMEM((width, width), BF16),
+            pltpu.VMEM((width, width), BF16),
+            pltpu.VMEM((width, width), BF16),
+            pltpu.VMEM((heads, dh, nfeat), BF16),
+            pltpu.VMEM((nrows, width), BF16),
+            pltpu.VMEM((2, cols, width), BF16),
+            pltpu.VMEM((heads, nrows, nfeat), BF16),
+            pltpu.VMEM((nrows, width), F32),
+            pltpu.VMEM((nrows, width), F32),
+            pltpu.VMEM((nrows, width), BF16),
+            pltpu.VMEM((slabs, nfeat, LANES), F32),
+            pltpu.VMEM((LANES, nfeat), F32),
+            pltpu.VMEM((slabs, half, LANES), BF16),
+            pltpu.VMEM((slabs, half, LANES), BF16),
+            pltpu.VMEM((chips, slabs, piece, LANES), BF16),
+            pltpu.VMEM((chips, slabs, piece, LANES), BF16),
+            pltpu.VMEM((slabs, nfeat, LANES), BF16),
+            sem((6,)), sem((rows_here,)), sem((2,)), sem((2,)), sem((slabs,)), sem((slabs,)),
+            sem((ng, chips)), sem((ng, chips)), sem((ng, chips)), sem((ng, chips)),
+            sem((ng, chips)), sem((ng, chips)),
+        ],
+        compiler_params=pltpu.CompilerParams(
+            collective_id=0, has_side_effects=True, vmem_limit_bytes=60 * 1024 * 1024
+        ),
+    )(flat, w_query, w_key, w_value, w_out, omega, conv_kernel, norm_gain.reshape(1, width))
+    return out.reshape(tokens.shape)
+
+
+def layer(n, *args):
+    heads, dh, nfeat = args[5].shape
+    width = args[0].shape[2]
+    fits = (
+        n % 2 == 0 and nfeat % (n * SUB) == 0 and 2 * dh == LANES and heads == 12
+        and nfeat == 2 * LANES and width == heads * dh
+    )
+    return fused(n, *args) if fits else shards(*args)
+
+
 def solution(mesh):
     return jax.shard_map(
-        shards,
+        functools.partial(layer, mesh.shape["row"]),
         mesh=mesh,
         in_specs=(P(("parts", "row"), None, None), P(), P(), P(), P(), P(), P(), P()),
         out_specs=P(("parts", "row"), None, None),

time: 116 us -> 33.6 us (0.29)
  the two profiles are of different devices: /device:TPU:0 before, /device:TPU:1 now
where the time goes in v1:
time: 33.6 us; the launch traced here: 33.3 us
  Pallas kernels  30 us (89%)
  local copies, waits for them, and re-layouts  3.33 us (10%)
    pallas_call x1, Pallas kernels, fused(): pl.pallas_call(functools.partial(kernel, dims), out_shape=jax.ShapeDtypeS...  30 us
    unnamed x1, local copies, waits for them, and re-layouts  2.06 us
    reshape x1, local copies, waits for them, and re-layouts, fused(): norm_gain.reshape(1, width)  1.27 us

profile of v1, /device:TPU:1, one launch (start us, length us, event | category | flops | bytes accessed | tf_op | source)
XLA Modules:
  0.0 33.3 jit_solution(16093668358019322850)
XLA Ops:
  0.0 1.3 %reshape.10.gain_ref = f32[1,768]{1,0:T(1,128)} reshape(f32[768]{0:T(1024)} %param.15) | data formatting | bytes 6144 | tf_op jit(solution)/shard_map/reshape | solution.py:389
  1.3 30.0 %shard_map.82 = bf16[512,768]{1,0:T(8,128)(2,1)} custom-call(bf16[512,768]{1,0:T(8,128)(2,1)} %bitcast.3, bf16[768,768]{1,0:T(8,128)(2,1)} %wq_hbm.1, bf16[768,768]{1,0:T(8,128)(2,1)} %wk_hbm.1, bf16[768,768]{1,0:T(8,128)(2,1)} %wv_hbm.1, bf16[768,768]{1,0:T(8,128)(2,1)} %wo_hbm.1, bf16[12,64,256]{2,1,0:T(8,128)(2,1)} %om_hbm.1, f32[3,3,768]{2,1,0:T(4,128)} %conv_ref.1, ...), custom_call_target="tpu_custom_call" | custom-call | tf_op jit(solution)/shard_map/pallas_call | solution.py:357
  31.3 2.1 %copy.10 = bf16[2,256,768]{2,1,0:T(8,128)(2,1)} copy(bf16[2,256,768]{2,1,0:T(8,128)(2,1)} %bitcast.2) | data formatting | bytes 1572864

commit v2 on v1

--- a/solution.py
+++ b/solution.py
@@ -318,7 +318,7 @@
     outs = []
     for r in range(rows_here):
         cut = slice(r * cols, (r + 1) * cols)
-        mixed = (att[cut] * scale[cut] * gain_ref[...] + pos[cut]).astype(BF16)
+        mixed = (att[cut] * scale[cut] * gain_ref[...].reshape(1, width) + pos[cut]).astype(BF16)
         outv[cut] = (tok[cut].astype(F32) + mm(mixed, wo[...])).astype(BF16)
         copy = pltpu.make_async_copy(outv.at[cut], out_hbm.at[cut], out_sem.at[r])
         copy.start()
@@ -386,7 +386,7 @@
         compiler_params=pltpu.CompilerParams(
             collective_id=0, has_side_effects=True, vmem_limit_bytes=60 * 1024 * 1024
         ),
-    )(flat, w_query, w_key, w_value, w_out, omega, conv_kernel, norm_gain.reshape(1, width))
+    )(flat, w_query, w_key, w_value, w_out, omega, conv_kernel, norm_gain)
     return out.reshape(tokens.shape)
 
 

time: 33.6 us -> 32.3 us (0.961)
  local copies, waits for them, and re-layouts: 3.33 us -> 2.06 us
    reshape x1 -> x0, local copies, waits for them, and re-layouts: 1.27 us -> none  [fused(): norm_gain.reshape(1, width)]
where the time goes in v2:
time: 32.3 us; the launch traced here: 32.1 us
  Pallas kernels  30 us (93%)
  local copies, waits for them, and re-layouts  2.06 us (6%)
    pallas_call x1, Pallas kernels, fused(): pl.pallas_call(functools.partial(kernel, dims), out_shape=jax.ShapeDtypeS...  30 us
    unnamed x1, local copies, waits for them, and re-layouts  2.06 us

profile of v2, /device:TPU:1, one launch (start us, length us, event | category | flops | bytes accessed | tf_op | source)
XLA Modules:
  0.0 32.1 jit_solution(9884486013634831165)
XLA Ops:
  0.0 30.0 %shard_map.82 = bf16[512,768]{1,0:T(8,128)(2,1)} custom-call(bf16[512,768]{1,0:T(8,128)(2,1)} %bitcast.3, bf16[768,768]{1,0:T(8,128)(2,1)} %wq_hbm.1, bf16[768,768]{1,0:T(8,128)(2,1)} %wk_hbm.1, bf16[768,768]{1,0:T(8,128)(2,1)} %wv_hbm.1, bf16[768,768]{1,0:T(8,128)(2,1)} %wo_hbm.1, bf16[12,64,256]{2,1,0:T(8,128)(2,1)} %om_hbm.1, f32[3,3,768]{2,1,0:T(4,128)} %conv_ref.1, ...), custom_call_target="tpu_custom_call" | custom-call | tf_op jit(solution)/shard_map/pallas_call | solution.py:357
  30.0 2.1 %copy.10 = bf16[2,256,768]{2,1,0:T(8,128)(2,1)} copy(bf16[2,256,768]{2,1,0:T(8,128)(2,1)} %bitcast.2) | data formatting | bytes 1572864
